TPU v7x, 32 devices: a whole 2x2x4 slice. The times are simulated.
32 devices in a mesh: rows: 4 (over z), cols: 4 (over x, core), rep: 2 (over y).
Axes of the slice: x: 2, y: 2, z: 4, core: 2. Of those that a mesh axis runs over, the one named last changes fastest.
Arguments:
- matrix: float32 [16384, 8192], P(('rep', 'rows'), 'cols'), parts along dimension 0, may hold values from -0.0625 to 0.0625
- labels: int32 [16384], P(('rep', 'rows')), parts along dimension 0, may hold values from 0 to 1
- lambdas: float32 [64], P('rep'), parts along dimension 0, may hold values from 0.01 to 0.2
- x_prev: float32 [64, 8192], P('rep', 'cols'), parts along dimension 0, may hold values from -4 to 4
- w_prev: float32 [64, 8192], P('rep', 'cols'), parts along dimension 0, may hold values from -4 to 4
- p_prev: float32 [64, 8192], P('rep', 'cols'), parts along dimension 0, may hold values from -1.5 to 1.5
- z_prev: float32 [64, 8192], P('rep', 'rows'), parts along dimension 0, may hold values from -6 to 6
- u_prev: float32 [64, 8192], P('rep', 'rows'), parts along dimension 0, may hold values from -6 to 6
Outputs:
- coeffs: float32 [64, 8192], P('rep', 'cols'), parts along dimension 0
- sparse: float32 [64, 8192], P('rep', 'cols'), parts along dimension 0
- margins: float32 [64, 8192], P('rep', 'rows'), parts along dimension 0
- margin_dual: float32 [64, 8192], P('rep', 'rows'), parts along dimension 0
There are 2 independent parts, one for each index of `rep`. A program takes and returns all parts, laid end to end along the dimension named above; each array names one. Nothing has to cross between parts.
All inputs are finite; a program needn't handle non-finite values.
Results may differ from a plain program's by a relative error of at most 0.0003.
Values sent between devices are 32-bit elements; how exact they have to be, the bound alone decides.
A program may use at most 128 MiB of HBM per device.

v0:
```python
import jax
import jax.numpy as jnp
from jax import lax
from jax.sharding import PartitionSpec as P

ITERS = 2
CG_STEPS = 5
NEWTON_STEPS = 8
HIGH = lax.Precision.HIGHEST


def apply_rows(vec, matrix):
    return lax.dot_general(
        vec, matrix, (((1,), (1,)), ((), ())), precision=HIGH, preferred_element_type=jnp.float32
    )


def apply_cols(vec, matrix):
    return lax.dot_general(
        vec, matrix, (((1,), (0,)), ((), ())), precision=HIGH, preferred_element_type=jnp.float32
    )


def proximal(target, sign):
    margin = target
    for step in range(NEWTON_STEPS):
        grad = margin - target - sign * jax.nn.sigmoid(-sign * margin)
        hess = 1.0 + jax.nn.sigmoid(margin) * jax.nn.sigmoid(-margin)
        margin = margin - grad / hess
    return margin


def forward(vec, matrix):
    return lax.psum(apply_rows(vec, matrix), "cols")


def forward_with_norm(vec, matrix):
    return lax.psum((apply_rows(vec, matrix), jnp.sum(vec * vec, axis=1)), "cols")


def backward(vec, matrix):
    partial_sum = apply_cols(vec, matrix)
    return lax.psum(partial_sum, "rows")


def squared_norm(value):
    return lax.psum(jnp.sum(value * value, axis=1), "cols")


def cg_image(direction, matrix):
    mapped, dd_part = forward_with_norm(direction, matrix)
    sq_part = jnp.sum(mapped * mapped, axis=1)
    back, sq_total = lax.psum((apply_cols(mapped, matrix), sq_part), "rows")
    curv_value = dd_part + sq_total
    return (direction + back, curv_value)


def local(matrix, labels, lambdas, x_prev, w_prev, p_prev, z_prev, u_prev):
    sign = (2.0 * labels.astype(jnp.float32) - 1.0)[None, :]
    coeffs, sparse, dual = (x_prev, w_prev, p_prev)
    margins, margin_dual = (z_prev, u_prev)
    for outer in range(ITERS):
        resid = (
            sparse
            - dual
            - coeffs
            + backward(margins - margin_dual - forward(coeffs, matrix), matrix)
        )
        direction = resid
        norm_now = squared_norm(resid)
        for step in range(CG_STEPS):
            image, curv_value = cg_image(direction, matrix)
            alpha = norm_now / curv_value
            coeffs = coeffs + alpha[:, None] * direction
            resid = resid - alpha[:, None] * image
            if step + 1 < CG_STEPS:
                norm_next = squared_norm(resid)
                direction = resid + (norm_next / norm_now)[:, None] * direction
                norm_now = norm_next
        target = forward(coeffs, matrix) + margin_dual
        margins = proximal(target, sign)
        margin_dual = target - margins
        total = coeffs + dual
        sparse = jnp.sign(total) * jnp.maximum(jnp.abs(total) - lambdas[:, None], 0.0)
        dual = total - sparse
    return (coeffs, sparse, margins, margin_dual)


def solution(mesh):
    return jax.shard_map(
        local,
        mesh=mesh,
        in_specs=(
            P(("rep", "rows"), "cols"),
            P(("rep", "rows")),
            P("rep"),
            P("rep", "cols"),
            P("rep", "cols"),
            P("rep", "cols"),
            P("rep", "rows"),
            P("rep", "rows"),
        ),
        out_specs=(P("rep", "cols"), P("rep", "cols"), P("rep", "rows"), P("rep", "rows")),
        check_vma=False,
    )
```

profile of v0, /device:TPU:0, one launch (start us, length us, event | category | flops | bytes accessed | tf_op | source)
XLA Modules:
  0.0 1297.5 jit_solution(16217579853619619662)
XLA Ops:
  7.3 19.3 %fusion.16 = f32[32,2048]{1,0:T(8,128)} fusion(f32[32,2048]{1,0:T(8,128)} %param.11, f32[2048,2048]{1,0:T(8,128)} %param.8), kind=kOutput, calls=%fused_computation.80 | convolution fusion | flops 1610612736 | bytes 17301504 | tf_op jit(solution)/shard_map/dot_general | solution.py:13
  26.6 35.1 %all-reduce.24.cloned.1.call-done = f32[32,2048]{1,0:T(8,128)} async-done(((f32[32,2048]{1,0:T(8,128)}), f32[32,2048]{1,0:T(8,128)}) %all-reduce.24.cloned.1.call-update) | async-done | bytes 262160 | tf_op jit(solution)/shard_map/psum | solution.py:34
  61.8 13.8 %fusion.4 = f32[32,2048]{1,0:T(8,128)} fusion(f32[2048,2048]{1,0:T(8,128)} %param.8, f32[32,2048]{1,0:T(8,128)} %all-reduce.24.cloned.1.call-done, f32[32,2048]{1,0:T(8,128)S(1)} %copy-done.14, f32[32,2048]{1,0:T(8,128)S(1)} %copy-done.3), kind=kOutput, calls=%fused_computation.57 | convolution fusion | flops 1610743808 | bytes 17825792 | tf_op jit(solution)/shard_map/dot_general | solution.py:19
  75.8 35.3 %all-reduce.26.cloned.1.call-done = f32[32,2048]{1,0:T(8,128)} async-done(((f32[32,2048]{1,0:T(8,128)}), f32[32,2048]{1,0:T(8,128)}) %all-reduce.26.cloned.1.call-update) | async-done | bytes 262160 | tf_op jit(solution)/shard_map/psum | solution.py:43
  112.3 19.2 %fusion.17 = f32[32,2048]{1,0:T(8,128)} fusion(f32[32,2048]{1,0:T(8,128)S(1)} %get-tuple-element.32, f32[2048,2048]{1,0:T(8,128)} %param.8), kind=kOutput, calls=%fused_computation.81 | convolution fusion | flops 1610612736 | bytes 17301504 | tf_op jit(solution)/shard_map/dot_general | solution.py:13
  137.2 26.6 %all-reduce.28.cloned.1.call-done = f32[32,2048]{1,0:T(8,128)} async-done(((f32[32,2048]{1,0:T(8,128)}), f32[32,2048]{1,0:T(8,128)}) %all-reduce.28.cloned.1.call-update) | async-done | bytes 262160 | tf_op jit(solution)/shard_map/psum | solution.py:38
  163.8 15.9 %fusion.18 = f32[32,2048]{1,0:T(8,128)} fusion(f32[32,2048]{1,0:T(8,128)} %all-reduce.28.cloned.1.call-done, f32[2048,2048]{1,0:T(8,128)} %param.8), kind=kOutput, calls=%fused_computation.82 | convolution fusion | flops 1610612736 | bytes 17301504 | tf_op jit(solution)/shard_map/dot_general | solution.py:19
  191.7 23.6 %all-reduce.30.cloned.1.call-done = f32[32,2048]{1,0:T(8,128)} async-done(((f32[32,2048]{1,0:T(8,128)}), f32[32,2048]{1,0:T(8,128)}) %all-reduce.30.cloned.1.call-update) | async-done | bytes 262160 | tf_op jit(solution)/shard_map/psum | solution.py:53
  222.6 19.9 %fusion.10 = f32[32,2048]{1,0:T(8,128)} fusion(f32[2048,2048]{1,0:T(8,128)} %param.8, f32[32,2048]{1,0:T(8,128)S(1)} %get-tuple-element.32, f32[32]{0:T(128)S(1)} %div.247, f32[32,2048]{1,0:T(8,128)} %all-reduce.30.cloned.1.call-done, f32[32]{0:T(128)S(1)} %add_divide_fusion.1), kind=kOutput, calls=%fused_computation.75 | convolution fusion | flops 1610940416 | bytes 17563904 | tf_op jit(solution)/shard_map/dot_general | solution.py:13
  249.4 25.7 %all-reduce.32.cloned.1.call-done = f32[32,2048]{1,0:T(8,128)} async-done(((f32[32,2048]{1,0:T(8,128)}), f32[32,2048]{1,0:T(8,128)}) %all-reduce.32.cloned.1.call-update) | async-done | bytes 262160 | tf_op jit(solution)/shard_map/psum | solution.py:38
  275.1 15.9 %fusion.19 = f32[32,2048]{1,0:T(8,128)} fusion(f32[32,2048]{1,0:T(8,128)} %all-reduce.32.cloned.1.call-done, f32[2048,2048]{1,0:T(8,128)} %param.8), kind=kOutput, calls=%fused_computation.83 | convolution fusion | flops 1610612736 | bytes 17301504 | tf_op jit(solution)/shard_map/dot_general | solution.py:19
  303.0 23.6 %all-reduce.34.cloned.1.call-done = f32[32,2048]{1,0:T(8,128)} async-done(((f32[32,2048]{1,0:T(8,128)}), f32[32,2048]{1,0:T(8,128)}) %all-reduce.34.cloned.1.call-update) | async-done | bytes 262160 | tf_op jit(solution)/shard_map/psum | solution.py:53
  333.9 19.2 %fusion.20 = f32[32,2048]{1,0:T(8,128)} fusion(f32[32,2048]{1,0:T(8,128)S(1)} %get-tuple-element.28, f32[2048,2048]{1,0:T(8,128)} %param.8), kind=kOutput, calls=%fused_computation.84 | convolution fusion | flops 1610612736 | bytes 17301504 | tf_op jit(solution)/shard_map/dot_general | solution.py:13
  359.7 25.9 %all-reduce.36.cloned.1.call-done = f32[32,2048]{1,0:T(8,128)} async-done(((f32[32,2048]{1,0:T(8,128)}), f32[32,2048]{1,0:T(8,128)}) %all-reduce.36.cloned.1.call-update) | async-done | bytes 262160 | tf_op jit(solution)/shard_map/psum | solution.py:38
  385.6 15.9 %fusion.21 = f32[32,2048]{1,0:T(8,128)} fusion(f32[32,2048]{1,0:T(8,128)} %all-reduce.36.cloned.1.call-done, f32[2048,2048]{1,0:T(8,128)} %param.8), kind=kOutput, calls=%fused_computation.85 | convolution fusion | flops 1610612736 | bytes 17301504 | tf_op jit(solution)/shard_map/dot_general | solution.py:19
  413.6 23.6 %all-reduce.38.cloned.1.call-done = f32[32,2048]{1,0:T(8,128)} async-done(((f32[32,2048]{1,0:T(8,128)}), f32[32,2048]{1,0:T(8,128)}) %all-reduce.38.cloned.1.call-update) | async-done | bytes 262160 | tf_op jit(solution)/shard_map/psum | solution.py:53
  444.4 19.2 %fusion.22 = f32[32,2048]{1,0:T(8,128)} fusion(f32[32,2048]{1,0:T(8,128)S(1)} %get-tuple-element.24, f32[2048,2048]{1,0:T(8,128)} %param.8), kind=kOutput, calls=%fused_computation.86 | convolution fusion | flops 1610612736 | bytes 17301504 | tf_op jit(solution)/shard_map/dot_general | solution.py:13
  470.3 25.9 %all-reduce.40.cloned.1.call-done = f32[32,2048]{1,0:T(8,128)} async-done(((f32[32,2048]{1,0:T(8,128)}), f32[32,2048]{1,0:T(8,128)}) %all-reduce.40.cloned.1.call-update) | async-done | bytes 262160 | tf_op jit(solution)/shard_map/psum | solution.py:38
  496.2 15.9 %fusion.23 = f32[32,2048]{1,0:T(8,128)} fusion(f32[32,2048]{1,0:T(8,128)} %all-reduce.40.cloned.1.call-done, f32[2048,2048]{1,0:T(8,128)} %param.8), kind=kOutput, calls=%fused_computation.87 | convolution fusion | flops 1610612736 | bytes 17301504 | tf_op jit(solution)/shard_map/dot_general | solution.py:19
  524.1 23.6 %all-reduce.42.cloned.1.call-done = f32[32,2048]{1,0:T(8,128)} async-done(((f32[32,2048]{1,0:T(8,128)}), f32[32,2048]{1,0:T(8,128)}) %all-reduce.42.cloned.1.call-update) | async-done | bytes 262160 | tf_op jit(solution)/shard_map/psum | solution.py:53
  554.8 20.0 %fusion.7 = f32[32,2048]{1,0:T(8,128)} fusion(f32[2048,2048]{1,0:T(8,128)} %param.8, f32[32,2048]{1,0:T(8,128)S(1)} %get-tuple-element.22, f32[32,2048]{1,0:T(8,128)S(1)} %get-tuple-element.24, f32[32]{0:T(128)S(1)} %div.253), kind=kOutput, calls=%fused_computation.61 | convolution fusion | flops 1610743808 | bytes 17563776 | tf_op jit(solution)/shard_map/dot_general | solution.py:13
  581.7 25.7 %all-reduce.44.cloned.1.call-done = f32[32,2048]{1,0:T(8,128)} async-done(((f32[32,2048]{1,0:T(8,128)}), f32[32,2048]{1,0:T(8,128)}) %all-reduce.44.cloned.1.call-update) | async-done | bytes 262160 | tf_op jit(solution)/shard_map/psum | solution.py:38
  608.4 12.2 psum.390
  620.9 19.2 %fusion.24 = f32[32,2048]{1,0:T(8,128)} fusion(f32[32,2048]{1,0:T(8,128)S(1)} %multiply_add_fusion.5, f32[2048,2048]{1,0:T(8,128)} %param.8), kind=kOutput, calls=%fused_computation.88 | convolution fusion | flops 1610612736 | bytes 17301504 | tf_op jit(solution)/shard_map/dot_general | solution.py:13
  640.3 29.4 %all-reduce.46.cloned.1.call-done = f32[32,2048]{1,0:T(8,128)} async-done(((f32[32,2048]{1,0:T(8,128)}), f32[32,2048]{1,0:T(8,128)}) %all-reduce.46.cloned.1.call-update) | async-done | bytes 262160 | tf_op jit(solution)/shard_map/psum | solution.py:34
  670.7 18.1 %fusion = f32[32,2048]{1,0:T(8,128)} fusion(f32[2048,2048]{1,0:T(8,128)} %param.8, f32[32,2048]{1,0:T(8,128)} %all-reduce.46.cloned.1.call-done, f32[32,2048]{1,0:T(8,128)S(1)} %add.444, f32[2048]{0:T(1024)S(1)} %get-tuple-element.34, f32[2048]{0:T(1024)S(1)} %get-tuple-element.33), kind=kOutput, calls=%fused_computation.26 | convolution fusion | flops 1619197952 | bytes 17580032 | tf_op jit(solution)/shard_map/dot_general | solution.py:19
  689.1 35.3 %all-reduce.48.cloned.1.call-done = f32[32,2048]{1,0:T(8,128)} async-done(((f32[32,2048]{1,0:T(8,128)}), f32[32,2048]{1,0:T(8,128)}) %all-reduce.48.cloned.1.call-update) | async-done | bytes 262160 | tf_op jit(solution)/shard_map/psum | solution.py:43
  725.7 19.2 %fusion.25 = f32[32,2048]{1,0:T(8,128)} fusion(f32[32,2048]{1,0:T(8,128)S(1)} %get-tuple-element.19, f32[2048,2048]{1,0:T(8,128)} %param.8), kind=kOutput, calls=%fused_computation.89 | convolution fusion | flops 1610612736 | bytes 17301504 | tf_op jit(solution)/shard_map/dot_general | solution.py:13
  750.6 26.6 %all-reduce.50.cloned.1.call-done = f32[32,2048]{1,0:T(8,128)} async-done(((f32[32,2048]{1,0:T(8,128)}), f32[32,2048]{1,0:T(8,128)}) %all-reduce.50.cloned.1.call-update) | async-done | bytes 262160 | tf_op jit(solution)/shard_map/psum | solution.py:38
  777.2 15.9 %fusion.26 = f32[32,2048]{1,0:T(8,128)} fusion(f32[32,2048]{1,0:T(8,128)} %all-reduce.50.cloned.1.call-done, f32[2048,2048]{1,0:T(8,128)} %param.8), kind=kOutput, calls=%fused_computation.90 | convolution fusion | flops 1610612736 | bytes 17301504 | tf_op jit(solution)/shard_map/dot_general | solution.py:19
  805.1 23.6 %all-reduce.52.cloned.1.call-done = f32[32,2048]{1,0:T(8,128)} async-done(((f32[32,2048]{1,0:T(8,128)}), f32[32,2048]{1,0:T(8,128)}) %all-reduce.52.cloned.1.call-update) | async-done | bytes 262160 | tf_op jit(solution)/shard_map/psum | solution.py:53
  836.0 19.9 %fusion.11 = f32[32,2048]{1,0:T(8,128)} fusion(f32[2048,2048]{1,0:T(8,128)} %param.8, f32[32,2048]{1,0:T(8,128)S(1)} %get-tuple-element.19, f32[32]{0:T(128)S(1)} %div.288, f32[32,2048]{1,0:T(8,128)} %all-reduce.52.cloned.1.call-done, f32[32]{0:T(128)S(1)} %add_divide_fusion), kind=kOutput, calls=%fused_computation.76 | convolution fusion | flops 1610940416 | bytes 17563904 | tf_op jit(solution)/shard_map/dot_general | solution.py:13
  862.8 25.7 %all-reduce.54.cloned.1.call-done = f32[32,2048]{1,0:T(8,128)} async-done(((f32[32,2048]{1,0:T(8,128)}), f32[32,2048]{1,0:T(8,128)}) %all-reduce.54.cloned.1.call-update) | async-done | bytes 262160 | tf_op jit(solution)/shard_map/psum | solution.py:38
  888.5 15.9 %fusion.27 = f32[32,2048]{1,0:T(8,128)} fusion(f32[32,2048]{1,0:T(8,128)} %all-reduce.54.cloned.1.call-done, f32[2048,2048]{1,0:T(8,128)} %param.8), kind=kOutput, calls=%fused_computation.91 | convolution fusion | flops 1610612736 | bytes 17301504 | tf_op jit(solution)/shard_map/dot_general | solution.py:19
  916.4 23.6 %all-reduce.56.cloned.1.call-done = f32[32,2048]{1,0:T(8,128)} async-done(((f32[32,2048]{1,0:T(8,128)}), f32[32,2048]{1,0:T(8,128)}) %all-reduce.56.cloned.1.call-update) | async-done | bytes 262160 | tf_op jit(solution)/shard_map/psum | solution.py:53
  947.3 19.2 %fusion.28 = f32[32,2048]{1,0:T(8,128)} fusion(f32[32,2048]{1,0:T(8,128)S(1)} %get-tuple-element.15, f32[2048,2048]{1,0:T(8,128)} %param.8), kind=kOutput, calls=%fused_computation.92 | convolution fusion | flops 1610612736 | bytes 17301504 | tf_op jit(solution)/shard_map/dot_general | solution.py:13
  973.1 25.9 %all-reduce.58.cloned.1.call-done = f32[32,2048]{1,0:T(8,128)} async-done(((f32[32,2048]{1,0:T(8,128)}), f32[32,2048]{1,0:T(8,128)}) %all-reduce.58.cloned.1.call-update) | async-done | bytes 262160 | tf_op jit(solution)/shard_map/psum | solution.py:38
  999.0 15.9 %fusion.29 = f32[32,2048]{1,0:T(8,128)} fusion(f32[32,2048]{1,0:T(8,128)} %all-reduce.58.cloned.1.call-done, f32[2048,2048]{1,0:T(8,128)} %param.8), kind=kOutput, calls=%fused_computation.93 | convolution fusion | flops 1610612736 | bytes 17301504 | tf_op jit(solution)/shard_map/dot_general | solution.py:19
  1027.0 23.6 %all-reduce.60.cloned.1.call-done = f32[32,2048]{1,0:T(8,128)} async-done(((f32[32,2048]{1,0:T(8,128)}), f32[32,2048]{1,0:T(8,128)}) %all-reduce.60.cloned.1.call-update) | async-done | bytes 262160 | tf_op jit(solution)/shard_map/psum | solution.py:53
  1057.8 19.2 %fusion.30 = f32[32,2048]{1,0:T(8,128)} fusion(f32[32,2048]{1,0:T(8,128)S(1)} %get-tuple-element.11, f32[2048,2048]{1,0:T(8,128)} %param.8), kind=kOutput, calls=%fused_computation.94 | convolution fusion | flops 1610612736 | bytes 17301504 | tf_op jit(solution)/shard_map/dot_general | solution.py:13
  1083.7 25.9 %all-reduce.62.cloned.1.call-done = f32[32,2048]{1,0:T(8,128)} async-done(((f32[32,2048]{1,0:T(8,128)}), f32[32,2048]{1,0:T(8,128)}) %all-reduce.62.cloned.1.call-update) | async-done | bytes 262160 | tf_op jit(solution)/shard_map/psum | solution.py:38
  1109.6 15.9 %fusion.31 = f32[32,2048]{1,0:T(8,128)} fusion(f32[32,2048]{1,0:T(8,128)} %all-reduce.62.cloned.1.call-done, f32[2048,2048]{1,0:T(8,128)} %param.8), kind=kOutput, calls=%fused_computation.95 | convolution fusion | flops 1610612736 | bytes 17301504 | tf_op jit(solution)/shard_map/dot_general | solution.py:19
  1137.5 23.8 %all-reduce.64.cloned.1.call-done = f32[32,2048]{1,0:T(8,128)} async-done(((f32[32,2048]{1,0:T(8,128)}), f32[32,2048]{1,0:T(8,128)}) %all-reduce.64.cloned.1.call-update) | async-done | bytes 262160 | tf_op jit(solution)/shard_map/psum | solution.py:53
  1168.4 20.0 %fusion.8 = f32[32,2048]{1,0:T(8,128)} fusion(f32[2048,2048]{1,0:T(8,128)} %param.8, f32[32,2048]{1,0:T(8,128)S(1)} %get-tuple-element.9, f32[32,2048]{1,0:T(8,128)S(1)} %get-tuple-element.11, f32[32]{0:T(128)S(1)} %div.294), kind=kOutput, calls=%fused_computation.62 | convolution fusion | flops 1610743808 | bytes 17563776 | tf_op jit(solution)/shard_map/dot_general | solution.py:13
  1195.2 25.7 %all-reduce.66.cloned.1.call-done = f32[32,2048]{1,0:T(8,128)} async-done(((f32[32,2048]{1,0:T(8,128)}), f32[32,2048]{1,0:T(8,128)}) %all-reduce.66.cloned.1.call-update) | async-done | bytes 262160 | tf_op jit(solution)/shard_map/psum | solution.py:38
  1222.0 12.0 psum.415
  1235.1 19.3 %fusion.32 = f32[32,2048]{1,0:T(8,128)} fusion(f32[32,2048]{1,0:T(8,128)S(1)} %get-tuple-element.7, f32[2048,2048]{1,0:T(8,128)} %param.8), kind=kOutput, calls=%fused_computation.96 | convolution fusion | flops 1610612736 | bytes 17301504 | tf_op jit(solution)/shard_map/dot_general | solution.py:13
  1254.4 29.7 %all-reduce.68.cloned.1.call-done = f32[32,2048]{1,0:T(8,128)} async-done(((f32[32,2048]{1,0:T(8,128)}), f32[32,2048]{1,0:T(8,128)}) %all-reduce.68.cloned.1.call-update) | async-done | bytes 262160 | tf_op jit(solution)/shard_map/psum | solution.py:34
  (159 shorter events, 233.4 us)
Async XLA Ops:
  7.2 104.0 %copy-start.2 = (f32[32,2048]{1,0:T(8,128)S(1)}, f32[32,2048]{1,0:T(8,128)}, u32[]{:S(2)}) copy-start(f32[32,2048]{1,0:T(8,128)} %param.11) | copy-start | bytes 786436
  7.2 54.6 %copy-start.14 = (f32[32,2048]{1,0:T(8,128)S(1)}, f32[32,2048]{1,0:T(8,128)}, u32[]{:S(2)}) copy-start(f32[32,2048]{1,0:T(8,128)} %param.14) | copy-start | bytes 786436
  7.2 54.6 %copy-start.3 = (f32[32,2048]{1,0:T(8,128)S(1)}, f32[32,2048]{1,0:T(8,128)}, u32[]{:S(2)}) copy-start(f32[32,2048]{1,0:T(8,128)} %param.15) | copy-start | bytes 786436
  7.2 104.0 %copy-start.15 = (f32[32,2048]{1,0:T(8,128)S(1)}, f32[32,2048]{1,0:T(8,128)}, u32[]{:S(2)}) copy-start(f32[32,2048]{1,0:T(8,128)} %param.12) | copy-start | bytes 786436
  7.2 103.9 %copy-start.13 = (f32[32,2048]{1,0:T(8,128)S(1)}, f32[32,2048]{1,0:T(8,128)}, u32[]{:S(2)}) copy-start(f32[32,2048]{1,0:T(8,128)} %param.13) | copy-start | bytes 786436
  7.2 54.6 %all-reduce.24.cloned.1.call-start = ((), (), s32[]{:S(2)}) async-start(), calls=%async_computation | async-start | bytes 524288 | tf_op jit(solution)/shard_map/psum | solution.py:34
  26.6 84.5 %all-reduce.26.cloned.1.call-start = ((), (), s32[]{:S(2)}) async-start(), calls=%async_computation.1 | async-start | bytes 524288 | tf_op jit(solution)/shard_map/psum | solution.py:43
  75.6 88.2 %all-reduce.28.cloned.1.call-start = ((), (), s32[]{:S(2)}) async-start(), calls=%async_computation.2 | async-start | bytes 524288 | tf_op jit(solution)/shard_map/psum | solution.py:38
  131.5 83.8 %all-reduce.30.cloned.1.call-start = ((), (), s32[]{:S(2)}) async-start(), calls=%async_computation.3 | async-start | bytes 524288 | tf_op jit(solution)/shard_map/psum | solution.py:53
  163.8 16.0 %copy-start.5 = (f32[32,2048]{1,0:T(8,128)S(1)}, f32[32,2048]{1,0:T(8,128)}, u32[]{:S(2)}) copy-start(f32[32,2048]{1,0:T(8,128)} %all-reduce.28.cloned.1.call-done) | copy-start | bytes 786436
  179.7 95.4 %all-reduce.32.cloned.1.call-start = ((), (), s32[]{:S(2)}) async-start(), calls=%async_computation.4 | async-start | bytes 524288 | tf_op jit(solution)/shard_map/psum | solution.py:38
  215.3 27.3 %copy-start.1 = (f32[32,2048]{1,0:T(8,128)S(1)}, f32[32,2048]{1,0:T(8,128)}, u32[]{:S(2)}) copy-start(f32[32,2048]{1,0:T(8,128)} %all-reduce.30.cloned.1.call-done) | copy-start | bytes 786436
  242.5 84.1 %all-reduce.34.cloned.1.call-start = ((), (), s32[]{:S(2)}) async-start(), calls=%async_computation.5 | async-start | bytes 524288 | tf_op jit(solution)/shard_map/psum | solution.py:53
  275.1 16.0 %copy-start.6 = (f32[32,2048]{1,0:T(8,128)S(1)}, f32[32,2048]{1,0:T(8,128)}, u32[]{:S(2)}) copy-start(f32[32,2048]{1,0:T(8,128)} %all-reduce.32.cloned.1.call-done) | copy-start | bytes 786436
  291.0 94.6 %all-reduce.36.cloned.1.call-start = ((), (), s32[]{:S(2)}) async-start(), calls=%async_computation.6 | async-start | bytes 524288 | tf_op jit(solution)/shard_map/psum | solution.py:38
  353.1 84.1 %all-reduce.38.cloned.1.call-start = ((), (), s32[]{:S(2)}) async-start(), calls=%async_computation.7 | async-start | bytes 524288 | tf_op jit(solution)/shard_map/psum | solution.py:53
  385.6 16.0 %copy-start.7 = (f32[32,2048]{1,0:T(8,128)S(1)}, f32[32,2048]{1,0:T(8,128)}, u32[]{:S(2)}) copy-start(f32[32,2048]{1,0:T(8,128)} %all-reduce.36.cloned.1.call-done) | copy-start | bytes 786436
  401.6 94.6 %all-reduce.40.cloned.1.call-start = ((), (), s32[]{:S(2)}) async-start(), calls=%async_computation.8 | async-start | bytes 524288 | tf_op jit(solution)/shard_map/psum | solution.py:38
  463.6 84.1 %all-reduce.42.cloned.1.call-start = ((), (), s32[]{:S(2)}) async-start(), calls=%async_computation.9 | async-start | bytes 524288 | tf_op jit(solution)/shard_map/psum | solution.py:53
  496.2 16.0 %copy-start.8 = (f32[32,2048]{1,0:T(8,128)S(1)}, f32[32,2048]{1,0:T(8,128)}, u32[]{:S(2)}) copy-start(f32[32,2048]{1,0:T(8,128)} %all-reduce.40.cloned.1.call-done) | copy-start | bytes 786436
  512.1 95.2 %all-reduce.44.cloned.1.call-start = ((), (), s32[]{:S(2)}) async-start(), calls=%async_computation.10 | async-start | bytes 524288 | tf_op jit(solution)/shard_map/psum | solution.py:38
  554.8 85.5 %copy-start.16 = (s32[2048]{0:T(1024)S(1)}, s32[2048]{0:T(1024)}, u32[]{:S(2)}) copy-start(s32[2048]{0:T(1024)} %param.9) | copy-start | bytes 24580
  574.8 94.9 %all-reduce.46.cloned.1.call-start = ((), (), s32[]{:S(2)}) async-start(), calls=%async_computation.11 | async-start | bytes 524288 | tf_op jit(solution)/shard_map/psum | solution.py:34
  640.1 84.4 %all-reduce.48.cloned.1.call-start = ((), (), s32[]{:S(2)}) async-start(), calls=%async_computation.12 | async-start | bytes 524288 | tf_op jit(solution)/shard_map/psum | solution.py:43
  670.7 53.7 %copy-start.17 = (f32[32]{0:T(128)S(1)}, f32[32]{0:T(128)}, u32[]{:S(2)}) copy-start(f32[32]{0:T(128)} %param.10) | copy-start | bytes 388
  688.9 88.3 %all-reduce.50.cloned.1.call-start = ((), (), s32[]{:S(2)}) async-start(), calls=%async_computation.13 | async-start | bytes 524288 | tf_op jit(solution)/shard_map/psum | solution.py:38
  744.9 83.8 %all-reduce.52.cloned.1.call-start = ((), (), s32[]{:S(2)}) async-start(), calls=%async_computation.14 | async-start | bytes 524288 | tf_op jit(solution)/shard_map/psum | solution.py:53
  777.2 16.0 %copy-start.12 = (f32[32,2048]{1,0:T(8,128)S(1)}, f32[32,2048]{1,0:T(8,128)}, u32[]{:S(2)}) copy-start(f32[32,2048]{1,0:T(8,128)} %all-reduce.50.cloned.1.call-done) | copy-start | bytes 786436
  793.1 95.4 %all-reduce.54.cloned.1.call-start = ((), (), s32[]{:S(2)}) async-start(), calls=%async_computation.15 | async-start | bytes 524288 | tf_op jit(solution)/shard_map/psum | solution.py:38
  828.7 27.3 %copy-start = (f32[32,2048]{1,0:T(8,128)S(1)}, f32[32,2048]{1,0:T(8,128)}, u32[]{:S(2)}) copy-start(f32[32,2048]{1,0:T(8,128)} %all-reduce.52.cloned.1.call-done) | copy-start | bytes 786436
  855.9 84.1 %all-reduce.56.cloned.1.call-start = ((), (), s32[]{:S(2)}) async-start(), calls=%async_computation.16 | async-start | bytes 524288 | tf_op jit(solution)/shard_map/psum | solution.py:53
  888.5 16.0 %copy-start.9 = (f32[32,2048]{1,0:T(8,128)S(1)}, f32[32,2048]{1,0:T(8,128)}, u32[]{:S(2)}) copy-start(f32[32,2048]{1,0:T(8,128)} %all-reduce.54.cloned.1.call-done) | copy-start | bytes 786436
  904.4 94.6 %all-reduce.58.cloned.1.call-start = ((), (), s32[]{:S(2)}) async-start(), calls=%async_computation.17 | async-start | bytes 524288 | tf_op jit(solution)/shard_map/psum | solution.py:38
  966.5 84.1 %all-reduce.60.cloned.1.call-start = ((), (), s32[]{:S(2)}) async-start(), calls=%async_computation.18 | async-start | bytes 524288 | tf_op jit(solution)/shard_map/psum | solution.py:53
  999.0 16.0 %copy-start.10 = (f32[32,2048]{1,0:T(8,128)S(1)}, f32[32,2048]{1,0:T(8,128)}, u32[]{:S(2)}) copy-start(f32[32,2048]{1,0:T(8,128)} %all-reduce.58.cloned.1.call-done) | copy-start | bytes 786436
  1015.0 94.6 %all-reduce.62.cloned.1.call-start = ((), (), s32[]{:S(2)}) async-start(), calls=%async_computation.19 | async-start | bytes 524288 | tf_op jit(solution)/shard_map/psum | solution.py:38
  1077.0 84.2 %all-reduce.64.cloned.1.call-start = ((), (), s32[]{:S(2)}) async-start(), calls=%async_computation.20 | async-start | bytes 524288 | tf_op jit(solution)/shard_map/psum | solution.py:53
  1109.6 16.0 %copy-start.11 = (f32[32,2048]{1,0:T(8,128)S(1)}, f32[32,2048]{1,0:T(8,128)}, u32[]{:S(2)}) copy-start(f32[32,2048]{1,0:T(8,128)} %all-reduce.62.cloned.1.call-done) | copy-start | bytes 786436
  1125.5 95.4 %all-reduce.66.cloned.1.call-start = ((), (), s32[]{:S(2)}) async-start(), calls=%async_computation.21 | async-start | bytes 524288 | tf_op jit(solution)/shard_map/psum | solution.py:38
  1188.3 95.8 %all-reduce.68.cloned.1.call-start = ((), (), s32[]{:S(2)}) async-start(), calls=%async_computation.22 | async-start | bytes 524288 | tf_op jit(solution)/shard_map/psum | solution.py:34
  1235.1 55.3 %copy-start.4 = (f32[32,2048]{1,0:T(8,128)}, f32[32,2048]{1,0:T(8,128)S(1)}, u32[]{:S(2)}) copy-start(f32[32,2048]{1,0:T(8,128)S(1)} %get-tuple-element.7) | copy-start | bytes 786436
Sparse Core Ops, SparseCore 0:
  26.7 35.0 all-reduce.23
  75.7 35.3 all-reduce.25
  131.6 32.1 all-reduce.27
  179.8 35.3 all-reduce.29
  242.6 32.4 all-reduce.31
  291.1 35.3 all-reduce.33
  353.2 32.3 all-reduce.35
  401.7 35.3 all-reduce.37
  463.8 32.3 all-reduce.39
  512.3 35.4 all-reduce.41
  574.9 32.4 all-reduce.43
  640.2 29.4 all-reduce.45
  689.0 35.3 all-reduce.47
  745.0 32.1 all-reduce.49
  793.2 35.3 all-reduce.51
  856.0 32.4 all-reduce.53
  904.5 35.3 all-reduce.55
  966.6 32.3 all-reduce.57
  1015.1 35.3 all-reduce.59
  1077.2 32.3 all-reduce.61
  1125.7 35.5 all-reduce.63
  1188.5 32.4 all-reduce.65
  1254.6 29.4 all-reduce.67
where the time goes:
time: 1310 us; the launch traced here: 1300 us
  waiting for transfers between devices  614 us (47%)
  matrix products  412 us (31%)
  blocking collectives  230 us (18%)
  other arithmetic  25.7 us (2%)
  between operations  14.8 us (1%)
    psum x10, waiting for transfers between devices, forward_with_norm(): lax.psum((apply_rows(vec, matrix), jnp.sum(vec * vec, axis=1)), 'cols')  260 us
    dot_general x13, matrix products, apply_rows(): lax.dot_general(vec, matrix, (((1,), (1,)), ((), ())), precision=HIGH, pr...  253 us
    psum x8, waiting for transfers between devices, cg_image(): back, sq_total = lax.psum((apply_cols(mapped, matrix), sq_part), 'rows')  189 us
    dot_general x10, matrix products, apply_cols(): lax.dot_general(vec, matrix, (((1,), (0,)), ((), ())), precision=HIGH, pr...  159 us
    psum x10, blocking collectives, cg_image(): back, sq_total = lax.psum((apply_cols(mapped, matrix), sq_part), 'rows')  118 us
    psum x3, waiting for transfers between devices, forward(): return lax.psum(apply_rows(vec, matrix), 'cols')  94.2 us
    psum x2, waiting for transfers between devices, backward(): return lax.psum(partial_sum, 'rows')  70.6 us
    psum x10, blocking collectives, squared_norm(): return lax.psum(jnp.sum(value * value, axis=1), 'cols')  58.7 us
  transfers between devices with their start and end apart: 23, of which 23 were waited for; matrix products, arithmetic and copies ran while one was open for 0% of the time, Pallas kernels for 0%

commit v1 on v0

--- a/solution.py
+++ b/solution.py
@@ -31,7 +31,7 @@
 
 
 def forward(vec, matrix):
-    return lax.psum(apply_rows(vec, matrix), "cols")
+    return jnp.sum(lax.all_gather(apply_rows(vec, matrix), "cols"), axis=0)
 
 
 def forward_with_norm(vec, matrix):

time: 1310 us -> 1260 us (0.962)
  waiting for transfers between devices: 614 us -> 567 us
    psum x3 -> x0, waiting for transfers between devices: 94.2 us -> none  [forward(): return lax.psum(apply_rows(vec, matrix), 'cols')]
    all_gather x0 -> x3, waiting for transfers between devices: none -> 47.6 us  [forward(): return jnp.sum(lax.all_gather(apply_rows(vec, matrix), 'cols'), axis=0)]
where the time goes in v1:
time: 1260 us; the launch traced here: 1250 us
  waiting for transfers between devices  567 us (45%)
  matrix products  410 us (33%)
  blocking collectives  230 us (18%)
  other arithmetic  27.8 us (2%)
  between operations  14.5 us (1%)
    psum x10, waiting for transfers between devices, forward_with_norm(): lax.psum((apply_rows(vec, matrix), jnp.sum(vec * vec, axis=1)), 'cols')  260 us
    dot_general x13, matrix products, apply_rows(): lax.dot_general(vec, matrix, (((1,), (1,)), ((), ())), precision=HIGH, pr...  253 us
    psum x8, waiting for transfers between devices, cg_image(): back, sq_total = lax.psum((apply_cols(mapped, matrix), sq_part), 'rows')  189 us
    dot_general x10, matrix products, apply_cols(): lax.dot_general(vec, matrix, (((1,), (0,)), ((), ())), precision=HIGH, pr...  157 us
    psum x10, blocking collectives, cg_image(): back, sq_total = lax.psum((apply_cols(mapped, matrix), sq_part), 'rows')  118 us
    psum x2, waiting for transfers between devices, backward(): return lax.psum(partial_sum, 'rows')  70.9 us
    psum x10, blocking collectives, squared_norm(): return lax.psum(jnp.sum(value * value, axis=1), 'cols')  58.7 us
    psum x8, blocking collectives, forward_with_norm(): lax.psum((apply_rows(vec, matrix), jnp.sum(vec * vec, axis=1)), 'cols')  52.8 us
  transfers between devices with their start and end apart: 23, of which 23 were waited for; matrix products, arithmetic and copies ran while one was open for 0% of the time, Pallas kernels for 0%

profile of v1, /device:TPU:0, one launch (start us, length us, event | category | flops | bytes accessed | tf_op | source)
XLA Modules:
  0.0 1250.6 jit_solution(2646658225080401726)
XLA Ops:
  7.3 19.3 %fusion.16 = f32[32,2048]{1,0:T(8,128)} fusion(f32[32,2048]{1,0:T(8,128)} %param.11, f32[2048,2048]{1,0:T(8,128)} %param.8), kind=kOutput, calls=%fused_computation.80 | convolution fusion | flops 1610612736 | bytes 17301504 | tf_op jit(solution)/shard_map/dot_general | solution.py:13
  26.6 19.5 %all-gather.7.cloned.1.call-done = f32[128,2048]{1,0:T(8,128)} async-done(((f32[32,2048]{1,0:T(8,128)}), f32[128,2048]{1,0:T(8,128)}) %all-gather.7.cloned.1.call-update) | async-done | bytes 1048592 | tf_op jit(solution)/shard_map/all_gather | solution.py:34
  47.5 13.8 %fusion.4 = f32[32,2048]{1,0:T(8,128)} fusion(f32[2048,2048]{1,0:T(8,128)} %param.8, f32[32,2048]{1,0:T(8,128)S(1)} %reduce_sum.291, f32[32,2048]{1,0:T(8,128)S(1)} %copy-done.14, f32[32,2048]{1,0:T(8,128)S(1)} %copy-done.3), kind=kOutput, calls=%fused_computation.57 | convolution fusion | flops 1610743808 | bytes 17825792 | tf_op jit(solution)/shard_map/dot_general | solution.py:19
  61.6 35.5 %all-reduce.21.cloned.1.call-done = f32[32,2048]{1,0:T(8,128)} async-done(((f32[32,2048]{1,0:T(8,128)}), f32[32,2048]{1,0:T(8,128)}) %all-reduce.21.cloned.1.call-update) | async-done | bytes 262160 | tf_op jit(solution)/shard_map/psum | solution.py:43
  98.2 19.2 %fusion.17 = f32[32,2048]{1,0:T(8,128)} fusion(f32[32,2048]{1,0:T(8,128)S(1)} %get-tuple-element.32, f32[2048,2048]{1,0:T(8,128)} %param.8), kind=kOutput, calls=%fused_computation.81 | convolution fusion | flops 1610612736 | bytes 17301504 | tf_op jit(solution)/shard_map/dot_general | solution.py:13
  123.1 26.6 %all-reduce.23.cloned.1.call-done = f32[32,2048]{1,0:T(8,128)} async-done(((f32[32,2048]{1,0:T(8,128)}), f32[32,2048]{1,0:T(8,128)}) %all-reduce.23.cloned.1.call-update) | async-done | bytes 262160 | tf_op jit(solution)/shard_map/psum | solution.py:38
  149.7 15.9 %fusion.18 = f32[32,2048]{1,0:T(8,128)} fusion(f32[32,2048]{1,0:T(8,128)} %all-reduce.23.cloned.1.call-done, f32[2048,2048]{1,0:T(8,128)} %param.8), kind=kOutput, calls=%fused_computation.82 | convolution fusion | flops 1610612736 | bytes 17301504 | tf_op jit(solution)/shard_map/dot_general | solution.py:19
  177.6 23.6 %all-reduce.25.cloned.1.call-done = f32[32,2048]{1,0:T(8,128)} async-done(((f32[32,2048]{1,0:T(8,128)}), f32[32,2048]{1,0:T(8,128)}) %all-reduce.25.cloned.1.call-update) | async-done | bytes 262160 | tf_op jit(solution)/shard_map/psum | solution.py:53
  208.6 19.9 %fusion.10 = f32[32,2048]{1,0:T(8,128)} fusion(f32[2048,2048]{1,0:T(8,128)} %param.8, f32[32,2048]{1,0:T(8,128)S(1)} %get-tuple-element.32, f32[32]{0:T(128)S(1)} %div.247, f32[32,2048]{1,0:T(8,128)} %all-reduce.25.cloned.1.call-done, f32[32]{0:T(128)S(1)} %add_divide_fusion.1), kind=kOutput, calls=%fused_computation.75 | convolution fusion | flops 1610940416 | bytes 17563904 | tf_op jit(solution)/shard_map/dot_general | solution.py:13
  235.4 25.7 %all-reduce.27.cloned.1.call-done = f32[32,2048]{1,0:T(8,128)} async-done(((f32[32,2048]{1,0:T(8,128)}), f32[32,2048]{1,0:T(8,128)}) %all-reduce.27.cloned.1.call-update) | async-done | bytes 262160 | tf_op jit(solution)/shard_map/psum | solution.py:38
  261.1 15.9 %fusion.19 = f32[32,2048]{1,0:T(8,128)} fusion(f32[32,2048]{1,0:T(8,128)} %all-reduce.27.cloned.1.call-done, f32[2048,2048]{1,0:T(8,128)} %param.8), kind=kOutput, calls=%fused_computation.83 | convolution fusion | flops 1610612736 | bytes 17301504 | tf_op jit(solution)/shard_map/dot_general | solution.py:19
  289.0 23.6 %all-reduce.29.cloned.1.call-done = f32[32,2048]{1,0:T(8,128)} async-done(((f32[32,2048]{1,0:T(8,128)}), f32[32,2048]{1,0:T(8,128)}) %all-reduce.29.cloned.1.call-update) | async-done | bytes 262160 | tf_op jit(solution)/shard_map/psum | solution.py:53
  319.9 19.2 %fusion.20 = f32[32,2048]{1,0:T(8,128)} fusion(f32[32,2048]{1,0:T(8,128)S(1)} %get-tuple-element.28, f32[2048,2048]{1,0:T(8,128)} %param.8), kind=kOutput, calls=%fused_computation.84 | convolution fusion | flops 1610612736 | bytes 17301504 | tf_op jit(solution)/shard_map/dot_general | solution.py:13
  345.7 25.9 %all-reduce.31.cloned.1.call-done = f32[32,2048]{1,0:T(8,128)} async-done(((f32[32,2048]{1,0:T(8,128)}), f32[32,2048]{1,0:T(8,128)}) %all-reduce.31.cloned.1.call-update) | async-done | bytes 262160 | tf_op jit(solution)/shard_map/psum | solution.py:38
  371.7 15.9 %fusion.21 = f32[32,2048]{1,0:T(8,128)} fusion(f32[32,2048]{1,0:T(8,128)} %all-reduce.31.cloned.1.call-done, f32[2048,2048]{1,0:T(8,128)} %param.8), kind=kOutput, calls=%fused_computation.85 | convolution fusion | flops 1610612736 | bytes 17301504 | tf_op jit(solution)/shard_map/dot_general | solution.py:19
  399.6 23.6 %all-reduce.33.cloned.1.call-done = f32[32,2048]{1,0:T(8,128)} async-done(((f32[32,2048]{1,0:T(8,128)}), f32[32,2048]{1,0:T(8,128)}) %all-reduce.33.cloned.1.call-update) | async-done | bytes 262160 | tf_op jit(solution)/shard_map/psum | solution.py:53
  430.6 19.2 %fusion.22 = f32[32,2048]{1,0:T(8,128)} fusion(f32[32,2048]{1,0:T(8,128)S(1)} %get-tuple-element.24, f32[2048,2048]{1,0:T(8,128)} %param.8), kind=kOutput, calls=%fused_computation.86 | convolution fusion | flops 1610612736 | bytes 17301504 | tf_op jit(solution)/shard_map/dot_general | solution.py:13
  456.5 25.9 %all-reduce.35.cloned.1.call-done = f32[32,2048]{1,0:T(8,128)} async-done(((f32[32,2048]{1,0:T(8,128)}), f32[32,2048]{1,0:T(8,128)}) %all-reduce.35.cloned.1.call-update) | async-done | bytes 262160 | tf_op jit(solution)/shard_map/psum | solution.py:38
  482.4 15.9 %fusion.23 = f32[32,2048]{1,0:T(8,128)} fusion(f32[32,2048]{1,0:T(8,128)} %all-reduce.35.cloned.1.call-done, f32[2048,2048]{1,0:T(8,128)} %param.8), kind=kOutput, calls=%fused_computation.87 | convolution fusion | flops 1610612736 | bytes 17301504 | tf_op jit(solution)/shard_map/dot_general | solution.py:19
  510.3 23.6 %all-reduce.37.cloned.1.call-done = f32[32,2048]{1,0:T(8,128)} async-done(((f32[32,2048]{1,0:T(8,128)}), f32[32,2048]{1,0:T(8,128)}) %all-reduce.37.cloned.1.call-update) | async-done | bytes 262160 | tf_op jit(solution)/shard_map/psum | solution.py:53
  540.8 20.0 %fusion.7 = f32[32,2048]{1,0:T(8,128)} fusion(f32[2048,2048]{1,0:T(8,128)} %param.8, f32[32,2048]{1,0:T(8,128)S(1)} %get-tuple-element.22, f32[32,2048]{1,0:T(8,128)S(1)} %get-tuple-element.24, f32[32]{0:T(128)S(1)} %div.253), kind=kOutput, calls=%fused_computation.61 | convolution fusion | flops 1610743808 | bytes 17563776 | tf_op jit(solution)/shard_map/dot_general | solution.py:13
  567.6 25.7 %all-reduce.39.cloned.1.call-done = f32[32,2048]{1,0:T(8,128)} async-done(((f32[32,2048]{1,0:T(8,128)}), f32[32,2048]{1,0:T(8,128)}) %all-reduce.39.cloned.1.call-update) | async-done | bytes 262160 | tf_op jit(solution)/shard_map/psum | solution.py:38
  594.4 11.9 psum.365
  606.5 19.2 %fusion.24 = f32[32,2048]{1,0:T(8,128)} fusion(f32[32,2048]{1,0:T(8,128)S(1)} %multiply_add_fusion.5, f32[2048,2048]{1,0:T(8,128)} %param.8), kind=kOutput, calls=%fused_computation.88 | convolution fusion | flops 1610612736 | bytes 17301504 | tf_op jit(solution)/shard_map/dot_general | solution.py:13
  625.8 14.0 %all-gather.9.cloned.1.call-done = f32[128,2048]{1,0:T(8,128)} async-done(((f32[32,2048]{1,0:T(8,128)}), f32[128,2048]{1,0:T(8,128)}) %all-gather.9.cloned.1.call-update) | async-done | bytes 1048592 | tf_op jit(solution)/shard_map/all_gather | solution.py:34
  641.2 15.9 %fusion = f32[32,2048]{1,0:T(8,128)} fusion(f32[2048,2048]{1,0:T(8,128)} %param.8, f32[32,2048]{1,0:T(8,128)S(1)} %reduce_sum.306, f32[32,2048]{1,0:T(8,128)S(1)} %add.437, f32[2048]{0:T(1024)S(1)} %get-tuple-element.34, f32[2048]{0:T(1024)S(1)} %get-tuple-element.33), kind=kOutput, calls=%fused_computation.26 | convolution fusion | flops 1619197952 | bytes 17580032 | tf_op jit(solution)/shard_map/dot_general | solution.py:19
  657.4 35.5 %all-reduce.41.cloned.1.call-done = f32[32,2048]{1,0:T(8,128)} async-done(((f32[32,2048]{1,0:T(8,128)}), f32[32,2048]{1,0:T(8,128)}) %all-reduce.41.cloned.1.call-update) | async-done | bytes 262160 | tf_op jit(solution)/shard_map/psum | solution.py:43
  694.1 19.2 %fusion.25 = f32[32,2048]{1,0:T(8,128)} fusion(f32[32,2048]{1,0:T(8,128)S(1)} %get-tuple-element.19, f32[2048,2048]{1,0:T(8,128)} %param.8), kind=kOutput, calls=%fused_computation.89 | convolution fusion | flops 1610612736 | bytes 17301504 | tf_op jit(solution)/shard_map/dot_general | solution.py:13
  719.1 26.6 %all-reduce.43.cloned.1.call-done = f32[32,2048]{1,0:T(8,128)} async-done(((f32[32,2048]{1,0:T(8,128)}), f32[32,2048]{1,0:T(8,128)}) %all-reduce.43.cloned.1.call-update) | async-done | bytes 262160 | tf_op jit(solution)/shard_map/psum | solution.py:38
  745.6 15.9 %fusion.26 = f32[32,2048]{1,0:T(8,128)} fusion(f32[32,2048]{1,0:T(8,128)} %all-reduce.43.cloned.1.call-done, f32[2048,2048]{1,0:T(8,128)} %param.8), kind=kOutput, calls=%fused_computation.90 | convolution fusion | flops 1610612736 | bytes 17301504 | tf_op jit(solution)/shard_map/dot_general | solution.py:19
  773.5 23.6 %all-reduce.45.cloned.1.call-done = f32[32,2048]{1,0:T(8,128)} async-done(((f32[32,2048]{1,0:T(8,128)}), f32[32,2048]{1,0:T(8,128)}) %all-reduce.45.cloned.1.call-update) | async-done | bytes 262160 | tf_op jit(solution)/shard_map/psum | solution.py:53
  804.4 19.9 %fusion.11 = f32[32,2048]{1,0:T(8,128)} fusion(f32[2048,2048]{1,0:T(8,128)} %param.8, f32[32,2048]{1,0:T(8,128)S(1)} %get-tuple-element.19, f32[32]{0:T(128)S(1)} %div.288, f32[32,2048]{1,0:T(8,128)} %all-reduce.45.cloned.1.call-done, f32[32]{0:T(128)S(1)} %add_divide_fusion), kind=kOutput, calls=%fused_computation.76 | convolution fusion | flops 1610940416 | bytes 17563904 | tf_op jit(solution)/shard_map/dot_general | solution.py:13
  831.2 25.7 %all-reduce.47.cloned.1.call-done = f32[32,2048]{1,0:T(8,128)} async-done(((f32[32,2048]{1,0:T(8,128)}), f32[32,2048]{1,0:T(8,128)}) %all-reduce.47.cloned.1.call-update) | async-done | bytes 262160 | tf_op jit(solution)/shard_map/psum | solution.py:38
  856.9 15.9 %fusion.27 = f32[32,2048]{1,0:T(8,128)} fusion(f32[32,2048]{1,0:T(8,128)} %all-reduce.47.cloned.1.call-done, f32[2048,2048]{1,0:T(8,128)} %param.8), kind=kOutput, calls=%fused_computation.91 | convolution fusion | flops 1610612736 | bytes 17301504 | tf_op jit(solution)/shard_map/dot_general | solution.py:19
  884.8 23.6 %all-reduce.49.cloned.1.call-done = f32[32,2048]{1,0:T(8,128)} async-done(((f32[32,2048]{1,0:T(8,128)}), f32[32,2048]{1,0:T(8,128)}) %all-reduce.49.cloned.1.call-update) | async-done | bytes 262160 | tf_op jit(solution)/shard_map/psum | solution.py:53
  915.7 19.2 %fusion.28 = f32[32,2048]{1,0:T(8,128)} fusion(f32[32,2048]{1,0:T(8,128)S(1)} %get-tuple-element.15, f32[2048,2048]{1,0:T(8,128)} %param.8), kind=kOutput, calls=%fused_computation.92 | convolution fusion | flops 1610612736 | bytes 17301504 | tf_op jit(solution)/shard_map/dot_general | solution.py:13
  941.6 25.9 %all-reduce.51.cloned.1.call-done = f32[32,2048]{1,0:T(8,128)} async-done(((f32[32,2048]{1,0:T(8,128)}), f32[32,2048]{1,0:T(8,128)}) %all-reduce.51.cloned.1.call-update) | async-done | bytes 262160 | tf_op jit(solution)/shard_map/psum | solution.py:38
  967.5 15.9 %fusion.29 = f32[32,2048]{1,0:T(8,128)} fusion(f32[32,2048]{1,0:T(8,128)} %all-reduce.51.cloned.1.call-done, f32[2048,2048]{1,0:T(8,128)} %param.8), kind=kOutput, calls=%fused_computation.93 | convolution fusion | flops 1610612736 | bytes 17301504 | tf_op jit(solution)/shard_map/dot_general | solution.py:19
  995.4 23.6 %all-reduce.53.cloned.1.call-done = f32[32,2048]{1,0:T(8,128)} async-done(((f32[32,2048]{1,0:T(8,128)}), f32[32,2048]{1,0:T(8,128)}) %all-reduce.53.cloned.1.call-update) | async-done | bytes 262160 | tf_op jit(solution)/shard_map/psum | solution.py:53
  1026.3 19.2 %fusion.30 = f32[32,2048]{1,0:T(8,128)} fusion(f32[32,2048]{1,0:T(8,128)S(1)} %get-tuple-element.11, f32[2048,2048]{1,0:T(8,128)} %param.8), kind=kOutput, calls=%fused_computation.94 | convolution fusion | flops 1610612736 | bytes 17301504 | tf_op jit(solution)/shard_map/dot_general | solution.py:13
  1052.1 25.9 %all-reduce.55.cloned.1.call-done = f32[32,2048]{1,0:T(8,128)} async-done(((f32[32,2048]{1,0:T(8,128)}), f32[32,2048]{1,0:T(8,128)}) %all-reduce.55.cloned.1.call-update) | async-done | bytes 262160 | tf_op jit(solution)/shard_map/psum | solution.py:38
  1078.1 15.9 %fusion.31 = f32[32,2048]{1,0:T(8,128)} fusion(f32[32,2048]{1,0:T(8,128)} %all-reduce.55.cloned.1.call-done, f32[2048,2048]{1,0:T(8,128)} %param.8), kind=kOutput, calls=%fused_computation.95 | convolution fusion | flops 1610612736 | bytes 17301504 | tf_op jit(solution)/shard_map/dot_general | solution.py:19
  1106.0 23.8 %all-reduce.57.cloned.1.call-done = f32[32,2048]{1,0:T(8,128)} async-done(((f32[32,2048]{1,0:T(8,128)}), f32[32,2048]{1,0:T(8,128)}) %all-reduce.57.cloned.1.call-update) | async-done | bytes 262160 | tf_op jit(solution)/shard_map/psum | solution.py:53
  1136.8 20.0 %fusion.8 = f32[32,2048]{1,0:T(8,128)} fusion(f32[2048,2048]{1,0:T(8,128)} %param.8, f32[32,2048]{1,0:T(8,128)S(1)} %get-tuple-element.9, f32[32,2048]{1,0:T(8,128)S(1)} %get-tuple-element.11, f32[32]{0:T(128)S(1)} %div.294), kind=kOutput, calls=%fused_computation.62 | convolution fusion | flops 1610743808 | bytes 17563776 | tf_op jit(solution)/shard_map/dot_general | solution.py:13
  1163.7 25.7 %all-reduce.59.cloned.1.call-done = f32[32,2048]{1,0:T(8,128)} async-done(((f32[32,2048]{1,0:T(8,128)}), f32[32,2048]{1,0:T(8,128)}) %all-reduce.59.cloned.1.call-update) | async-done | bytes 262160 | tf_op jit(solution)/shard_map/psum | solution.py:38
  1190.4 12.2 psum.389
  1203.8 19.3 %fusion.32 = f32[32,2048]{1,0:T(8,128)} fusion(f32[32,2048]{1,0:T(8,128)S(1)} %get-tuple-element.7, f32[2048,2048]{1,0:T(8,128)} %param.8), kind=kOutput, calls=%fused_computation.96 | convolution fusion | flops 1610612736 | bytes 17301504 | tf_op jit(solution)/shard_map/dot_general | solution.py:13
  1223.1 14.1 %all-gather.11.cloned.1.call-done = f32[128,2048]{1,0:T(8,128)} async-done(((f32[32,2048]{1,0:T(8,128)}), f32[128,2048]{1,0:T(8,128)}) %all-gather.11.cloned.1.call-update) | async-done | bytes 1048592 | tf_op jit(solution)/shard_map/all_gather | solution.py:34
  (162 shorter events, 235.4 us)
Async XLA Ops:
  7.2 89.9 %copy-start.2 = (f32[32,2048]{1,0:T(8,128)S(1)}, f32[32,2048]{1,0:T(8,128)}, u32[]{:S(2)}) copy-start(f32[32,2048]{1,0:T(8,128)} %param.11) | copy-start | bytes 786436
  7.2 40.3 %copy-start.14 = (f32[32,2048]{1,0:T(8,128)S(1)}, f32[32,2048]{1,0:T(8,128)}, u32[]{:S(2)}) copy-start(f32[32,2048]{1,0:T(8,128)} %param.14) | copy-start | bytes 786436
  7.2 40.3 %copy-start.3 = (f32[32,2048]{1,0:T(8,128)S(1)}, f32[32,2048]{1,0:T(8,128)}, u32[]{:S(2)}) copy-start(f32[32,2048]{1,0:T(8,128)} %param.15) | copy-start | bytes 786436
  7.2 89.9 %copy-start.15 = (f32[32,2048]{1,0:T(8,128)S(1)}, f32[32,2048]{1,0:T(8,128)}, u32[]{:S(2)}) copy-start(f32[32,2048]{1,0:T(8,128)} %param.12) | copy-start | bytes 786436
  7.2 89.9 %copy-start.13 = (f32[32,2048]{1,0:T(8,128)S(1)}, f32[32,2048]{1,0:T(8,128)}, u32[]{:S(2)}) copy-start(f32[32,2048]{1,0:T(8,128)} %param.13) | copy-start | bytes 786436
  7.2 39.0 %all-gather.7.cloned.1.call-start = ((), (), s32[]{:S(2)}) async-start(), calls=%async_computation.20 | async-start | bytes 1310720 | tf_op jit(solution)/shard_map/all_gather | solution.py:34
  26.6 70.5 %all-reduce.21.cloned.1.call-start = ((), (), s32[]{:S(2)}) async-start(), calls=%async_computation | async-start | bytes 524288 | tf_op jit(solution)/shard_map/psum | solution.py:43
  61.3 88.4 %all-reduce.23.cloned.1.call-start = ((), (), s32[]{:S(2)}) async-start(), calls=%async_computation.1 | async-start | bytes 524288 | tf_op jit(solution)/shard_map/psum | solution.py:38
  117.4 83.8 %all-reduce.25.cloned.1.call-start = ((), (), s32[]{:S(2)}) async-start(), calls=%async_computation.2 | async-start | bytes 524288 | tf_op jit(solution)/shard_map/psum | solution.py:53
  149.7 16.0 %copy-start.5 = (f32[32,2048]{1,0:T(8,128)S(1)}, f32[32,2048]{1,0:T(8,128)}, u32[]{:S(2)}) copy-start(f32[32,2048]{1,0:T(8,128)} %all-reduce.23.cloned.1.call-done) | copy-start | bytes 786436
  165.6 95.4 %all-reduce.27.cloned.1.call-start = ((), (), s32[]{:S(2)}) async-start(), calls=%async_computation.3 | async-start | bytes 524288 | tf_op jit(solution)/shard_map/psum | solution.py:38
  201.2 27.4 %copy-start.1 = (f32[32,2048]{1,0:T(8,128)S(1)}, f32[32,2048]{1,0:T(8,128)}, u32[]{:S(2)}) copy-start(f32[32,2048]{1,0:T(8,128)} %all-reduce.25.cloned.1.call-done) | copy-start | bytes 786436
  228.5 84.1 %all-reduce.29.cloned.1.call-start = ((), (), s32[]{:S(2)}) async-start(), calls=%async_computation.4 | async-start | bytes 524288 | tf_op jit(solution)/shard_map/psum | solution.py:53
  261.1 16.0 %copy-start.6 = (f32[32,2048]{1,0:T(8,128)S(1)}, f32[32,2048]{1,0:T(8,128)}, u32[]{:S(2)}) copy-start(f32[32,2048]{1,0:T(8,128)} %all-reduce.27.cloned.1.call-done) | copy-start | bytes 786436
  277.0 94.7 %all-reduce.31.cloned.1.call-start = ((), (), s32[]{:S(2)}) async-start(), calls=%async_computation.5 | async-start | bytes 524288 | tf_op jit(solution)/shard_map/psum | solution.py:38
  339.1 84.1 %all-reduce.33.cloned.1.call-start = ((), (), s32[]{:S(2)}) async-start(), calls=%async_computation.6 | async-start | bytes 524288 | tf_op jit(solution)/shard_map/psum | solution.py:53
  371.7 16.0 %copy-start.7 = (f32[32,2048]{1,0:T(8,128)S(1)}, f32[32,2048]{1,0:T(8,128)}, u32[]{:S(2)}) copy-start(f32[32,2048]{1,0:T(8,128)} %all-reduce.31.cloned.1.call-done) | copy-start | bytes 786436
  387.6 94.8 %all-reduce.35.cloned.1.call-start = ((), (), s32[]{:S(2)}) async-start(), calls=%async_computation.7 | async-start | bytes 524288 | tf_op jit(solution)/shard_map/psum | solution.py:38
  449.8 84.1 %all-reduce.37.cloned.1.call-start = ((), (), s32[]{:S(2)}) async-start(), calls=%async_computation.8 | async-start | bytes 524288 | tf_op jit(solution)/shard_map/psum | solution.py:53
  482.4 16.0 %copy-start.8 = (f32[32,2048]{1,0:T(8,128)S(1)}, f32[32,2048]{1,0:T(8,128)}, u32[]{:S(2)}) copy-start(f32[32,2048]{1,0:T(8,128)} %all-reduce.35.cloned.1.call-done) | copy-start | bytes 786436
  498.4 95.0 %all-reduce.39.cloned.1.call-start = ((), (), s32[]{:S(2)}) async-start(), calls=%async_computation.9 | async-start | bytes 524288 | tf_op jit(solution)/shard_map/psum | solution.py:38
  540.8 85.0 %copy-start.16 = (s32[2048]{0:T(1024)S(1)}, s32[2048]{0:T(1024)}, u32[]{:S(2)}) copy-start(s32[2048]{0:T(1024)} %param.9) | copy-start | bytes 24580
  560.8 79.1 %all-gather.9.cloned.1.call-start = ((), (), s32[]{:S(2)}) async-start(), calls=%async_computation.21 | async-start | bytes 1310720 | tf_op jit(solution)/shard_map/all_gather | solution.py:34
  625.7 67.2 %all-reduce.41.cloned.1.call-start = ((), (), s32[]{:S(2)}) async-start(), calls=%async_computation.10 | async-start | bytes 524288 | tf_op jit(solution)/shard_map/psum | solution.py:43
  641.2 51.7 %copy-start.17 = (f32[32]{0:T(128)S(1)}, f32[32]{0:T(128)}, u32[]{:S(2)}) copy-start(f32[32]{0:T(128)} %param.10) | copy-start | bytes 388
  657.1 88.5 %all-reduce.43.cloned.1.call-start = ((), (), s32[]{:S(2)}) async-start(), calls=%async_computation.11 | async-start | bytes 524288 | tf_op jit(solution)/shard_map/psum | solution.py:38
  713.3 83.8 %all-reduce.45.cloned.1.call-start = ((), (), s32[]{:S(2)}) async-start(), calls=%async_computation.12 | async-start | bytes 524288 | tf_op jit(solution)/shard_map/psum | solution.py:53
  745.6 16.0 %copy-start.12 = (f32[32,2048]{1,0:T(8,128)S(1)}, f32[32,2048]{1,0:T(8,128)}, u32[]{:S(2)}) copy-start(f32[32,2048]{1,0:T(8,128)} %all-reduce.43.cloned.1.call-done) | copy-start | bytes 786436
  761.6 95.4 %all-reduce.47.cloned.1.call-start = ((), (), s32[]{:S(2)}) async-start(), calls=%async_computation.13 | async-start | bytes 524288 | tf_op jit(solution)/shard_map/psum | solution.py:38
  797.1 27.3 %copy-start = (f32[32,2048]{1,0:T(8,128)S(1)}, f32[32,2048]{1,0:T(8,128)}, u32[]{:S(2)}) copy-start(f32[32,2048]{1,0:T(8,128)} %all-reduce.45.cloned.1.call-done) | copy-start | bytes 786436
  824.4 84.1 %all-reduce.49.cloned.1.call-start = ((), (), s32[]{:S(2)}) async-start(), calls=%async_computation.14 | async-start | bytes 524288 | tf_op jit(solution)/shard_map/psum | solution.py:53
  856.9 16.0 %copy-start.9 = (f32[32,2048]{1,0:T(8,128)S(1)}, f32[32,2048]{1,0:T(8,128)}, u32[]{:S(2)}) copy-start(f32[32,2048]{1,0:T(8,128)} %all-reduce.47.cloned.1.call-done) | copy-start | bytes 786436
  872.9 94.6 %all-reduce.51.cloned.1.call-start = ((), (), s32[]{:S(2)}) async-start(), calls=%async_computation.15 | async-start | bytes 524288 | tf_op jit(solution)/shard_map/psum | solution.py:38
  934.9 84.1 %all-reduce.53.cloned.1.call-start = ((), (), s32[]{:S(2)}) async-start(), calls=%async_computation.16 | async-start | bytes 524288 | tf_op jit(solution)/shard_map/psum | solution.py:53
  967.5 16.0 %copy-start.10 = (f32[32,2048]{1,0:T(8,128)S(1)}, f32[32,2048]{1,0:T(8,128)}, u32[]{:S(2)}) copy-start(f32[32,2048]{1,0:T(8,128)} %all-reduce.51.cloned.1.call-done) | copy-start | bytes 786436
  983.4 94.6 %all-reduce.55.cloned.1.call-start = ((), (), s32[]{:S(2)}) async-start(), calls=%async_computation.17 | async-start | bytes 524288 | tf_op jit(solution)/shard_map/psum | solution.py:38
  1045.5 84.2 %all-reduce.57.cloned.1.call-start = ((), (), s32[]{:S(2)}) async-start(), calls=%async_computation.18 | async-start | bytes 524288 | tf_op jit(solution)/shard_map/psum | solution.py:53
  1078.1 16.0 %copy-start.11 = (f32[32,2048]{1,0:T(8,128)S(1)}, f32[32,2048]{1,0:T(8,128)}, u32[]{:S(2)}) copy-start(f32[32,2048]{1,0:T(8,128)} %all-reduce.55.cloned.1.call-done) | copy-start | bytes 786436
  1094.0 95.4 %all-reduce.59.cloned.1.call-start = ((), (), s32[]{:S(2)}) async-start(), calls=%async_computation.19 | async-start | bytes 524288 | tf_op jit(solution)/shard_map/psum | solution.py:38
  1156.8 80.4 %all-gather.11.cloned.1.call-start = ((), (), s32[]{:S(2)}) async-start(), calls=%async_computation.22 | async-start | bytes 1310720 | tf_op jit(solution)/shard_map/all_gather | solution.py:34
  1203.8 40.1 %copy-start.4 = (f32[32,2048]{1,0:T(8,128)}, f32[32,2048]{1,0:T(8,128)S(1)}, u32[]{:S(2)}) copy-start(f32[32,2048]{1,0:T(8,128)S(1)} %get-tuple-element.7) | copy-start | bytes 786436
Sparse Core Ops, SparseCore 0:
  26.7 19.4 all-gather.6
  61.5 35.5 all-reduce.20
  117.5 32.1 all-reduce.22
  165.8 35.3 all-reduce.24
  228.6 32.3 all-reduce.26
  277.1 35.3 all-reduce.28
  339.2 32.4 all-reduce.30
  387.7 35.4 all-reduce.32
  450.0 32.4 all-reduce.34
  498.5 35.4 all-reduce.36
  560.9 32.4 all-reduce.38
  625.9 13.9 all-gather.8
  657.3 35.5 all-reduce.40
  713.5 32.1 all-reduce.42
  761.7 35.3 all-reduce.44
  824.5 32.4 all-reduce.46
  873.0 35.3 all-reduce.48
  935.1 32.3 all-reduce.50
  983.6 35.3 all-reduce.52
  1045.6 32.3 all-reduce.54
  1094.1 35.5 all-reduce.56
  1156.9 32.4 all-reduce.58
  1223.2 13.9 all-gather.10
